TPU v7x, 32 devices: a whole 2x2x4 slice. The times are simulated.
32 devices in a mesh: seq: 8 (over y, x, core), head: 4 (over z).
Axes of the slice: x: 2, y: 2, z: 4, core: 2. Of those that a mesh axis runs over, the one named last changes fastest.
Arguments:
- inputs: bfloat16 [2048, 4096], P('seq', 'head'), may hold values from -6 to 6
- gates: bfloat16 [2048, 4096], P('seq', 'head'), may hold values from -6 to 6
- b_proj: bfloat16 [2048, 128], P('seq'), may hold values from -6 to 6
- c_proj: bfloat16 [2048, 128], P('seq'), may hold values from -6 to 6
- step_size: float32 [64, 2048], P('head', 'seq'), may hold values from 0 to 2
- decay_rate: float32 [64], P('head'), may hold values from 0.5 to 2
- norm_gain: float32 [4096], P('head'), may hold values from 0.5 to 1.5
- out_weight: bfloat16 [4096, 4096], P('seq', 'head'), may hold values from -0.09375 to 0.09375
- grad_out: bfloat16 [2048, 4096], P('seq', 'head'), may hold values from -6 to 6
Outputs:
- grad_inputs: bfloat16 [2048, 4096], P('seq', 'head')
- grad_gates: bfloat16 [2048, 4096], P('seq', 'head')
- grad_b: float32 [2048, 128], P('seq')
- grad_c: float32 [2048, 128], P('seq')
- grad_step: float32 [64, 2048], P('head', 'seq')
- grad_rate: float32 [64], P('head')
- grad_gain: float32 [4096], P('head')
- grad_weight: float32 [4096, 4096], P('seq', 'head')
All inputs are finite; a program needn't handle non-finite values.
Results may differ from a plain program's by a relative error of at most 0.0042.
Values may be sent and summed in bfloat16 or wider, within the bound.
A program may use at most 64 MiB of HBM per device.

v0:
```python
import jax
import jax.numpy as jnp
from jax import lax
from jax.sharding import PartitionSpec as P

EPSILON = 1e-05


def carried_in(part, axis, combine, identity, reverse):
    count = lax.axis_size(axis)
    place = lax.axis_index(axis)
    ahead = count - 1 - place if reverse else place
    gathered = jax.tree.map(lambda a: lax.all_gather(a, axis), part)
    state = jax.tree.map(lambda a, e: jnp.zeros_like(a) + jnp.asarray(e, a.dtype), part, identity)

    def one(turn, state):
        source = count - 1 - turn if reverse else turn
        return combine(
            state, jax.tree.map(lambda a: lax.dynamic_index_in_dim(a, source, 0, False), gathered)
        )

    return lax.fori_loop(0, ahead, one, state)


def dot_high(left, right):
    return jnp.dot(left, right, precision=lax.Precision.HIGHEST, preferred_element_type=jnp.float32)


def dot_inner(left, right):
    return lax.dot_general(
        left,
        right,
        (((0,), (0,)), ((), ())),
        precision=lax.Precision.HIGHEST,
        preferred_element_type=jnp.float32,
    )


def decay_table(step, rate):
    logs = -jnp.cumsum(rate * step)
    count = step.shape[0]
    later = lax.broadcasted_iota(jnp.int32, (count, count), 0)
    earlier = lax.broadcasted_iota(jnp.int32, (count, count), 1)
    spread = jnp.minimum(logs[:, None] - logs[None, :], 0.0)
    table = jnp.where(later >= earlier, jnp.exp(spread), 0.0)
    return (logs, table)


def span_summary(step, rate, values, keys_b):
    logs = -jnp.cumsum(rate * step)
    tail = jnp.exp(logs[-1] - logs)
    return (jnp.exp(logs[-1]), dot_inner(keys_b * (step * tail)[:, None], values))


def span_output(step, rate, values, keys_b, queries_c, state_in):
    logs, table = decay_table(step, rate)
    scores = dot_high(queries_c, keys_b.T)
    mixing = table * scores * step[None, :]
    return dot_high(mixing, values) + jnp.exp(logs)[:, None] * dot_high(queries_c, state_in)


def adjoint_summary(step, rate, queries_c, grads):
    logs = -jnp.cumsum(rate * step)
    return (jnp.exp(logs[-1]), dot_inner(queries_c * jnp.exp(logs)[:, None], grads))


def span_backward(step, rate, values, keys_b, queries_c, grads, state_in, adjoint_in):
    logs, table = decay_table(step, rate)
    tail = jnp.exp(logs[-1] - logs)
    front = jnp.exp(logs)
    scores = dot_high(queries_c, keys_b.T)
    inner = dot_high(grads, values.T)
    weighted = table * inner
    mixing = table * scores * step[None, :]
    keys_adjoint = dot_high(keys_b, adjoint_in)
    grad_values = dot_inner(mixing, grads) + (step * tail)[:, None] * keys_adjoint
    grad_keys = step[:, None] * (
        dot_inner(weighted, queries_c) + tail[:, None] * dot_high(values, adjoint_in.T)
    )
    grad_queries = dot_high(weighted * step[None, :], keys_b) + front[:, None] * dot_high(
        grads, state_in.T
    )
    carried = tail * jnp.sum(keys_adjoint * values, axis=1)
    q_terms = jnp.sum(weighted * scores, axis=0) + carried
    row_part = jnp.sum(mixing * inner, axis=1) + front * jnp.sum(
        dot_high(queries_c, state_in) * grads, axis=1
    )
    drive = row_part - step * q_terms
    state_end = jnp.exp(logs[-1]) * state_in + dot_inner(keys_b * (step * tail)[:, None], values)
    boundary = jnp.sum(adjoint_in * state_end)
    log_grad = jnp.flip(jnp.cumsum(jnp.flip(drive))) + boundary
    grad_step = q_terms - rate * log_grad
    rate_part = -jnp.sum(step * log_grad)
    return (grad_values, grad_keys, grad_queries, grad_step, rate_part)


def combine(earlier, later):
    return (earlier[0] * later[0], later[1] + later[0][:, None, None] * earlier[1])


def on_device(
    inputs, gates, b_proj, c_proj, step_size, decay_rate, norm_gain, out_weight, grad_out
):
    length, width = inputs.shape
    heads = step_size.shape[0]
    head_width = width // heads
    values = inputs.astype(jnp.float32).reshape(length, heads, head_width).transpose(1, 0, 2)
    keys_b = b_proj.astype(jnp.float32)
    queries_c = c_proj.astype(jnp.float32)
    grad_full = lax.all_gather(grad_out, "head", axis=1, tiled=True)
    columns = grad_full
    grad_normed = jnp.dot(
        columns,
        lax.all_gather(out_weight, "seq", axis=0, tiled=True),
        preferred_element_type=jnp.float32,
    )
    decays, local_states = jax.vmap(span_summary, in_axes=(0, 0, 0, None))(
        step_size, decay_rate, values, keys_b
    )
    identity = (jnp.ones_like(decays), jnp.zeros_like(local_states))
    _, state_in = carried_in((decays, local_states), "seq", combine, identity, False)

    def output_head(items):
        step, rate, head_values, state = items
        return span_output(step, rate, head_values, keys_b, queries_c, state)

    head_out = lax.map(output_head, (step_size, decay_rate, values, state_in))
    ssd_out = head_out.transpose(1, 0, 2).reshape(length, width)
    gate_values = gates.astype(jnp.float32)
    sigmoid_gate = jax.nn.sigmoid(gate_values)
    gated = ssd_out * gate_values * sigmoid_gate
    total_width = width * lax.axis_size("head")
    scaled = grad_normed * norm_gain[None, :]
    squares = lax.psum(jnp.sum(gated * gated, axis=1), "head")
    cross = lax.psum(jnp.sum(scaled * gated, axis=1), "head")
    inv_rms = lax.rsqrt(squares / total_width + EPSILON)
    normed = (gated * inv_rms[:, None] * norm_gain[None, :]).astype(jnp.bfloat16)
    gain_part = jnp.sum(grad_normed * gated * inv_rms[:, None], axis=0)
    grad_gated = inv_rms[:, None] * (
        scaled - gated * (inv_rms * inv_rms * cross / total_width)[:, None]
    )
    grad_ssd = grad_gated * gate_values * sigmoid_gate
    grad_gates = (
        grad_gated * ssd_out * sigmoid_gate * (1.0 + gate_values * (1.0 - sigmoid_gate))
    ).astype(jnp.bfloat16)
    grads = grad_ssd.reshape(length, heads, head_width).transpose(1, 0, 2)
    back_decays, back_local = jax.vmap(adjoint_summary, in_axes=(0, 0, None, 0))(
        step_size, decay_rate, queries_c, grads
    )
    _, adjoint_in = carried_in((back_decays, back_local), "seq", combine, identity, True)

    def backward_head(items):
        step, rate, head_values, head_grads, state, adjoint = items
        return span_backward(step, rate, head_values, keys_b, queries_c, head_grads, state, adjoint)

    grad_values, grad_keys, grad_queries, grad_step, rate_part = lax.map(
        backward_head, (step_size, decay_rate, values, grads, state_in, adjoint_in)
    )
    grad_inputs = grad_values.transpose(1, 0, 2).reshape(length, width).astype(jnp.bfloat16)
    grad_b, grad_c = lax.psum((jnp.sum(grad_keys, axis=0), jnp.sum(grad_queries, axis=0)), "head")
    grad_gain, grad_rate = lax.psum((gain_part, rate_part), "seq")
    columns = grad_full
    grad_weight = lax.psum_scatter(
        lax.dot_general(
            columns, normed, (((0,), (0,)), ((), ())), preferred_element_type=jnp.float32
        ),
        "seq",
        scatter_dimension=0,
        tiled=True,
    )
    return (grad_inputs, grad_gates, grad_b, grad_c, grad_step, grad_rate, grad_gain, grad_weight)


def solution(mesh):
    in_specs = (
        P("seq", "head"),
        P("seq", "head"),
        P("seq", None),
        P("seq", None),
        P("head", "seq"),
        P("head"),
        P("head"),
        P("seq", "head"),
        P("seq", "head"),
    )
    out_specs = (
        P("seq", "head"),
        P("seq", "head"),
        P("seq", None),
        P("seq", None),
        P("head", "seq"),
        P("head"),
        P("head"),
        P("seq", "head"),
    )
    return jax.shard_map(
        on_device, mesh=mesh, in_specs=in_specs, out_specs=out_specs, check_vma=False
    )
```

profile of v0, /device:TPU:0, one launch (start us, length us, event | category | flops | bytes accessed | tf_op | source)
XLA Modules:
  0.0 613.4 jit_solution(8905541471411670778)
XLA Ops:
  12.0 2.0 fusion.76
  18.4 15.5 %all-reduce = f32[128]{0:T(128)S(1)} all-reduce(f32[128]{0:T(128)S(1)} %dynamic-update-slice), channel_id=3, replica_groups=mesh['seq'=8,'head'=4] {'seq'}, use_global_device_ids=true, to_apply=%add | all-reduce | flops 128 | bytes 1024
  34.0 19.5 %all-gather.12.cloned.1.call-done = f32[128,128,64]{1,2,0:T(8,128)} async-done(((f32[16,128,64]{1,2,0:T(8,128)}), f32[128,128,64]{1,2,0:T(8,128)}) %all-gather.12.cloned.1.call-update) | async-done | bytes 4194320 | tf_op jit(solution)/shard_map/all_gather | solution.py:13
  54.3 76.9 %while.62 = (s32[]{:T(128)}, f32[16,256,64]{1,2,0:T(8,128)}, f32[16]{0:T(128)S(1)}, f32[16,256]{1,0:T(8,128)}, f32[256,256]{1,0:T(8,128)S(1)}, /*index=5*/f32[16...) while((s32[]{:T(128)}, f32[16,256,64]{1,2,0:T(8,128)}, f32[16]{0:T(128)S(1)}, ...), condition=%wide.region_7.8_spmd.clone, body=%wide.region_4.7_spmd.sunk.clone | while | flops 75956736 | bytes 734393 | solution.py:127
  133.3 11.6 %psum.42 = f32[256]{0:T(256)S(1)} all-reduce(f32[256]{0:T(256)S(1)} %multiply_reduce_fusion.5), channel_id=1, replica_groups=mesh['seq'=8,'head'=4] {'head'}, use_global_device_ids=true, to_apply=%region_9.10 | all-reduce | flops 256 | bytes 2048 | tf_op jit(solution)/shard_map/psum | solution.py:134
  144.9 11.0 %all-gather.10.cloned.1.call-done = bf16[4096,1024]{1,0:T(8,128)(2,1)} async-done(((bf16[512,1024]{1,0:T(8,128)(2,1)}), bf16[4096,1024]{1,0:T(8,128)(2,1)}) %all-gather.10.cloned.1.call-update) | async-done | bytes 8388624 | tf_op jit(solution)/shard_map/all_gather | solution.py:114
  155.9 7.5 %multiply_reduce_fusion.3 = (f32[1024]{0:T(1024)S(1)}, f32[256]{0:T(256)S(1)}, f32[256,1024]{1,0:T(8,128)}) fusion(f32[256]{0:T(256)S(1)} %add_rsqrt_fusion, f32[256,1024]{1,0:T(8,128)S(1)} %copy.46, bf16[256,1024]{1,0:T(8,128)(2,1)S(1)} %copy-done.1, f32[1024]{0:T(1024)S(1)} %copy-done.8, bf16[256,4096]{1,0:T(8,128)(2,1)} %all-gather.8.cloned.1.call-done, ...), kind=kOutput, calls=%fused_computation.128 | convolution fusion | flops 2150628096 | bytes 13117440 | tf_op jit(solution)/shard_map/dot_general | solution.py:112
  163.4 11.6 %psum.43 = f32[256]{0:T(256)S(1)} all-reduce(f32[256]{0:T(256)S(1)} %get-tuple-element.503), channel_id=1, replica_groups=mesh['seq'=8,'head'=4] {'head'}, use_global_device_ids=true, to_apply=%region_11.12 | all-reduce | flops 256 | bytes 2048 | tf_op jit(solution)/shard_map/psum | solution.py:135
  175.1 3.1 fusion.85
  179.7 2.5 fusion.74
  184.5 10.1 %convolution_bitcast_fusion.2 = f32[4096,1024]{0,1:T(8,128)} fusion(bf16[256,4096]{1,0:T(8,128)(2,1)} %all-gather.8.cloned.1.call-done, f32[1024]{0:T(1024)S(1)} %copy-done.8, f32[256]{0:T(256)S(1)} %add_rsqrt_fusion, f32[256,1024]{1,0:T(8,128)S(1)} %copy.46, bf16[256,1024]{1,0:T(8,128)(2,1)} %param.18), kind=kOutput, calls=%fused_computation.110 | convolution fusion | flops 2149842944 | bytes 20452352 | tf_op jit(solution)/shard_map/dot_general | solution.py:164
  194.6 21.5 %all-gather.14.cloned.1.call-done = f32[128,128,64]{1,2,0:T(8,128)} async-done(((f32[16,128,64]{1,2,0:T(8,128)}), f32[128,128,64]{1,2,0:T(8,128)}) %all-gather.14.cloned.1.call-update) | async-done | bytes 4194320 | tf_op jit(solution)/shard_map/all_gather | solution.py:13
  216.3 12.1 %while.63 = (s32[]{:T(128)}, f32[16,128,64]{2,1,0:T(8,128)S(1)}, s32[]{:T(128)}, f32[8,16,128,64]{2,3,1,0:T(8,128)}, f32[8,16]{1,0:T(8,128)S(1)}) while((s32[]{:T(128)}, f32[16,128,64]{2,1,0:T(8,128)S(1)}, s32[]{:T(128)}, f32[8,16,128,64]{2,3,1,0:T(8,128)}, f32[8,16]{1,0:T(8,128)S(1)}) %tuple.185), condition=%wide.region_13.14_spmd.clone, body=%wide.region_12.13_spmd.sunk.clone | while | flops 262150 | bytes 3670331 | solution.py:22
  228.7 336.4 %while.64 = (s32[]{:T(128)}, bf16[16,256,64]{1,2,0:T(8,128)(2,1)S(1)}, f32[16,256,128]{2,1,0:T(8,128)}, f32[16,256,128]{2,1,0:T(8,128)}, f32[16,256]{1,0:T(8,128...) while((s32[]{:T(128)}, ...), condition=%wide.region_25.26_spmd.clone, body=%wide.region_14.25_spmd.sunk.clone | while | flops 430050560 | bytes 4782993 | solution.py:156
  238.9 1.8 fusion.192
  241.0 1.9 multiply_reduce_fusion.11
  259.9 1.7 fusion.192
  262.1 1.9 multiply_reduce_fusion.11
  281.0 1.7 fusion.192
  283.1 1.9 multiply_reduce_fusion.11
  302.0 1.7 fusion.192
  304.2 1.9 multiply_reduce_fusion.11
  323.1 1.7 fusion.192
  325.2 1.9 multiply_reduce_fusion.11
  344.1 1.7 fusion.192
  346.2 1.9 multiply_reduce_fusion.11
  365.1 1.7 fusion.192
  367.2 1.9 multiply_reduce_fusion.11
  386.1 1.7 fusion.192
  388.2 1.9 multiply_reduce_fusion.11
  407.1 1.7 fusion.192
  409.2 1.9 multiply_reduce_fusion.11
  428.1 1.7 fusion.192
  430.2 1.9 multiply_reduce_fusion.11
  451.2 1.9 multiply_reduce_fusion.11
  470.1 1.7 fusion.192
  472.2 1.9 multiply_reduce_fusion.11
  493.2 1.9 multiply_reduce_fusion.11
  512.1 1.7 fusion.192
  514.2 1.9 multiply_reduce_fusion.11
  533.1 1.7 fusion.192
  535.2 1.9 multiply_reduce_fusion.11
  554.1 1.7 fusion.192
  556.2 1.9 multiply_reduce_fusion.11
  565.1 2.5 reduce_sum.107
  568.4 12.7 %all-reduce.1 = (f32[16]{0:T(128)}, f32[1024]{0:T(1024)}) all-reduce(f32[16]{0:T(128)S(1)} %get-tuple-element.376, f32[1024]{0:T(1024)S(1)} %get-tuple-element.502), channel_id=1, replica_groups=mesh['seq'=8,'head'=4] {'seq'}, use_global_device_ids=true, to_apply=%region_30.31 | all-reduce | flops 1040 | bytes 8320 | tf_op jit(solution)/shard_map/psum | solution.py:161
  582.1 2.9 copy.53
  585.0 18.4 %all-reduce.5.cloned.1.call-done = (f32[256,128]{1,0:T(8,128)}, f32[256,128]{1,0:T(8,128)}) async-done(((f32[256,128]{1,0:T(8,128)}, f32[256,128]{1,0:T(8,128)}), (f32[256,128]{1,0:T(8,128)}, f32[256,128]{1,0:T(8,128)})) %all-reduce.5.cloned.1.call-update) | async-done | bytes 262160 | tf_op jit(solution)/shard_map/psum | solution.py:160
  (709 shorter events, 368.5 us)
Async XLA Ops:
  7.2 46.4 %all-gather.12.cloned.1.call-start = ((), (), s32[]{:S(2)}) async-start(), calls=%async_computation.4 | async-start | bytes 4718592 | tf_op jit(solution)/shard_map/all_gather | solution.py:13
  10.7 4.8 copy-start.6
  12.0 3.6 copy-start.7
  14.0 3.0 copy-start.10
  14.0 130.9 %all-gather.8.cloned.1.call-start = ((), (), s32[]{:S(2)}) async-start(), calls=%async_computation.1 | async-start | bytes 2621440 | tf_op jit(solution)/shard_map/all_gather | solution.py:110
  14.8 141.2 %all-gather.10.cloned.1.call-start = ((), (), s32[]{:S(2)}) async-start(), calls=%async_computation.2 | async-start | bytes 9437184 | tf_op jit(solution)/shard_map/all_gather | solution.py:114
  15.5 200.7 %all-gather.14.cloned.1.call-start = ((), (), s32[]{:S(2)}) async-start(), calls=%async_computation.5 | async-start | bytes 4718592 | tf_op jit(solution)/shard_map/all_gather | solution.py:13
  53.7 0.7 copy-start.9
  131.2 32.2 %copy-start.4 = (f32[256,256]{1,0:T(8,128)}, f32[256,256]{1,0:T(8,128)S(1)}, u32[]{:S(2)}) copy-start(f32[256,256]{1,0:T(8,128)S(1)} %get-tuple-element.1071) | copy-start | bytes 786436
  131.2 1.7 copy-start.1
  131.2 24.7 %copy-start.8 = (f32[1024]{0:T(1024)S(1)}, f32[1024]{0:T(1024)}, u32[]{:S(2)}) copy-start(f32[1024]{0:T(1024)} %param.23) | copy-start | bytes 12292
  179.7 4.8 copy-start
  182.2 399.9 %reduce-scatter.2.cloned.1.call-start = ((), (), s32[]{:S(2)}) async-start(), calls=%async_computation.3 | async-start | bytes 18874368 | tf_op jit(solution)/shard_map/reduce_scatter | solution.py:163
  194.6 408.8 %all-reduce.5.cloned.1.call-start = ((), (), s32[]{:S(2)}) async-start(), calls=%async_computation.6 | async-start | bytes 524288 | tf_op jit(solution)/shard_map/psum | solution.py:160
  216.3 12.4 %copy-start.3 = (bf16[16,256,64]{1,2,0:T(8,128)(2,1)S(1)}, bf16[16,256,64]{1,2,0:T(8,128)(2,1)}, u32[]{:S(2)}) copy-start(bf16[16,256,64]{1,2,0:T(8,128)(2,1)} %broadcast_convert_fusion) | copy-start | bytes 1572868
  228.7 17.5 %copy-start.5 = (f32[256,256]{1,0:T(8,128)S(1)}, f32[256,256]{1,0:T(8,128)}, u32[]{:S(2)}) copy-start(f32[256,256]{1,0:T(8,128)} %get-tuple-element.1027) | copy-start | bytes 786436 | tf_op jit(solution)/shard_map/while
  249.9 17.4 %copy-start.5 = (f32[256,256]{1,0:T(8,128)S(1)}, f32[256,256]{1,0:T(8,128)}, u32[]{:S(2)}) copy-start(f32[256,256]{1,0:T(8,128)} %get-tuple-element.1027) | copy-start | bytes 786436 | tf_op jit(solution)/shard_map/while
  271.0 17.4 %copy-start.5 = (f32[256,256]{1,0:T(8,128)S(1)}, f32[256,256]{1,0:T(8,128)}, u32[]{:S(2)}) copy-start(f32[256,256]{1,0:T(8,128)} %get-tuple-element.1027) | copy-start | bytes 786436 | tf_op jit(solution)/shard_map/while
  292.0 17.4 %copy-start.5 = (f32[256,256]{1,0:T(8,128)S(1)}, f32[256,256]{1,0:T(8,128)}, u32[]{:S(2)}) copy-start(f32[256,256]{1,0:T(8,128)} %get-tuple-element.1027) | copy-start | bytes 786436 | tf_op jit(solution)/shard_map/while
  313.1 17.3 %copy-start.5 = (f32[256,256]{1,0:T(8,128)S(1)}, f32[256,256]{1,0:T(8,128)}, u32[]{:S(2)}) copy-start(f32[256,256]{1,0:T(8,128)} %get-tuple-element.1027) | copy-start | bytes 786436 | tf_op jit(solution)/shard_map/while
  334.1 17.3 %copy-start.5 = (f32[256,256]{1,0:T(8,128)S(1)}, f32[256,256]{1,0:T(8,128)}, u32[]{:S(2)}) copy-start(f32[256,256]{1,0:T(8,128)} %get-tuple-element.1027) | copy-start | bytes 786436 | tf_op jit(solution)/shard_map/while
  355.1 17.3 %copy-start.5 = (f32[256,256]{1,0:T(8,128)S(1)}, f32[256,256]{1,0:T(8,128)}, u32[]{:S(2)}) copy-start(f32[256,256]{1,0:T(8,128)} %get-tuple-element.1027) | copy-start | bytes 786436 | tf_op jit(solution)/shard_map/while
  376.1 17.3 %copy-start.5 = (f32[256,256]{1,0:T(8,128)S(1)}, f32[256,256]{1,0:T(8,128)}, u32[]{:S(2)}) copy-start(f32[256,256]{1,0:T(8,128)} %get-tuple-element.1027) | copy-start | bytes 786436 | tf_op jit(solution)/shard_map/while
  397.1 17.3 %copy-start.5 = (f32[256,256]{1,0:T(8,128)S(1)}, f32[256,256]{1,0:T(8,128)}, u32[]{:S(2)}) copy-start(f32[256,256]{1,0:T(8,128)} %get-tuple-element.1027) | copy-start | bytes 786436 | tf_op jit(solution)/shard_map/while
  418.1 17.3 %copy-start.5 = (f32[256,256]{1,0:T(8,128)S(1)}, f32[256,256]{1,0:T(8,128)}, u32[]{:S(2)}) copy-start(f32[256,256]{1,0:T(8,128)} %get-tuple-element.1027) | copy-start | bytes 786436 | tf_op jit(solution)/shard_map/while
  439.1 17.3 %copy-start.5 = (f32[256,256]{1,0:T(8,128)S(1)}, f32[256,256]{1,0:T(8,128)}, u32[]{:S(2)}) copy-start(f32[256,256]{1,0:T(8,128)} %get-tuple-element.1027) | copy-start | bytes 786436 | tf_op jit(solution)/shard_map/while
  460.1 17.3 %copy-start.5 = (f32[256,256]{1,0:T(8,128)S(1)}, f32[256,256]{1,0:T(8,128)}, u32[]{:S(2)}) copy-start(f32[256,256]{1,0:T(8,128)} %get-tuple-element.1027) | copy-start | bytes 786436 | tf_op jit(solution)/shard_map/while
  481.1 17.3 %copy-start.5 = (f32[256,256]{1,0:T(8,128)S(1)}, f32[256,256]{1,0:T(8,128)}, u32[]{:S(2)}) copy-start(f32[256,256]{1,0:T(8,128)} %get-tuple-element.1027) | copy-start | bytes 786436 | tf_op jit(solution)/shard_map/while
  502.1 17.3 %copy-start.5 = (f32[256,256]{1,0:T(8,128)S(1)}, f32[256,256]{1,0:T(8,128)}, u32[]{:S(2)}) copy-start(f32[256,256]{1,0:T(8,128)} %get-tuple-element.1027) | copy-start | bytes 786436 | tf_op jit(solution)/shard_map/while
  523.1 17.3 %copy-start.5 = (f32[256,256]{1,0:T(8,128)S(1)}, f32[256,256]{1,0:T(8,128)}, u32[]{:S(2)}) copy-start(f32[256,256]{1,0:T(8,128)} %get-tuple-element.1027) | copy-start | bytes 786436 | tf_op jit(solution)/shard_map/while
  544.1 17.3 %copy-start.5 = (f32[256,256]{1,0:T(8,128)S(1)}, f32[256,256]{1,0:T(8,128)}, u32[]{:S(2)}) copy-start(f32[256,256]{1,0:T(8,128)} %get-tuple-element.1027) | copy-start | bytes 786436 | tf_op jit(solution)/shard_map/while
  565.1 2.5 copy-start.2
Sparse Core Ops, SparseCore 0:
  14.1 39.3 all-gather.11
  55.1 45.6 all-gather.7
  102.7 53.1 all-gather.9
  182.3 33.7 all-gather.13
  219.6 116.0 reduce-scatter.1
  568.5 34.8 all-reduce.4
where the time goes:
time: 623 us; the launch traced here: 613 us
  matrix products  245 us (39%)
  other arithmetic  118 us (19%)
  local copies, waits for them, and re-layouts  88.5 us (14%)
  waiting for transfers between devices  71.9 us (12%)
  blocking collectives  51.5 us (8%)
  loops' own time  22.8 us (4%)
  between operations  15 us (2%)
    dot_general x129, matrix products, dot_high(): jnp.dot(left, right, precision=lax.Precision.HIGHEST, preferred_element_t...  154 us
    dot_general x50, matrix products, dot_inner(): lax.dot_general(left, right, (((0,), (0,)), ((), ())), precision=lax.Prec...  73.7 us
    mul x32, other arithmetic, decay_table(): logs = -jnp.cumsum(rate * step)  43.3 us
    all_gather x2, waiting for transfers between devices, carried_in(): gathered = jax.tree.map(lambda a: lax.all_gather(a, axis), part)  41.1 us
    reduce_sum x16, other arithmetic, span_backward(): rate_part = -jnp.sum(step * log_grad)  30.3 us
    dynamic_update_slice x32, local copies, waits for them, and re-layouts, on_device(): lax.map(backward_head, (step_size, decay_rate, values, grads, state_in, a...  22.7 us
    another operation x1, loops' own time, on_device(): lax.map(backward_head, (step_size, decay_rate, values, grads, state_in, a...  22.3 us
    another operation x119, other arithmetic  19.2 us
  transfers between devices with their start and end apart: 6, of which 4 were waited for; matrix products, arithmetic and copies ran while one was open for 70% of the time, Pallas kernels for 0%

commit v1 on v0

v1 whole, which is shorter than its diff:
```python
import jax
import jax.numpy as jnp
from jax import lax
from jax.experimental import pallas as pl
from jax.experimental.pallas import tpu as pltpu
from jax.sharding import PartitionSpec as P

EPSILON = 1e-05
F32 = jnp.float32
BF16 = jnp.bfloat16


def split(a):
    high = a.astype(BF16)
    return high, (a - high.astype(F32)).astype(BF16)


def parts(a):
    high = lax.reduce_precision(a, 8, 7)
    return high.astype(BF16), (a - high).astype(BF16)


def dot_dims(left, right, dims):
    return lax.dot_general(left, right, (dims, ((), ())), preferred_element_type=F32)


def dot_exact_right(left, right, dims, split=parts):
    high, low = split(left)
    return dot_dims(high, right, dims) + dot_dims(low, right, dims)


def dot_exact_left(left, right, dims, split=parts):
    high, low = split(right)
    return dot_dims(left, high, dims) + dot_dims(left, low, dims)


def dot_both(left, right, dims, split=parts):
    left_high, left_low = split(left)
    right_high, right_low = split(right)
    return (
        dot_dims(left_high, right_high, dims)
        + dot_dims(left_high, right_low, dims)
        + dot_dims(left_low, right_high, dims)
    )


def dot_high(left, right, dims):
    return lax.dot_general(
        left, right, (dims, ((), ())), precision=lax.Precision.HIGHEST, preferred_element_type=F32
    )


ROW_COL = ((1,), (0,))
ROW_ROW = ((1,), (1,))
COL_COL = ((0,), (0,))


def forward_kernel(group, x_ref, keys_ref, scores_ref, step_row, log_row, step_col, log_col,
                   y_ref, front_ref, tail_ref, step_ref, state_ref):
    width = x_ref.shape[1] // group
    scores = scores_ref[...]
    outs, fronts, tails, steps = [], [], [], []
    for j in range(group):
        columns = log_col[0, :, j : j + 1]
        rows = log_row[0, j : j + 1, :]
        table = jnp.exp(jnp.minimum(columns - rows, 0.0))
        mixing = table * scores * step_row[0, j : j + 1, :]
        outs.append(dot_exact_right(mixing, x_ref[:, j * width : (j + 1) * width], ROW_COL, split))
        shape = (columns.shape[0], width)
        fronts.append(jnp.broadcast_to(jnp.exp(columns), shape))
        tails.append(jnp.broadcast_to(jnp.exp(columns[-1:, :] - columns), shape))
        steps.append(jnp.broadcast_to(step_col[0, :, j : j + 1], shape))
    tail = jnp.concatenate(tails, axis=1)
    step = jnp.concatenate(steps, axis=1)
    y_ref[...] = jnp.concatenate(outs, axis=1)
    front_ref[...] = jnp.concatenate(fronts, axis=1)
    tail_ref[...] = tail
    step_ref[...] = step
    weighted = x_ref[...].astype(F32) * (step * tail)
    state_ref[...] = dot_exact_left(keys_ref[...], weighted, COL_COL, split)


def backward_kernel(group, x_ref, e_ref, scores_ref, step_row, log_row, log_col, g_ref, m_ref):
    width = x_ref.shape[1] // group
    scores = scores_ref[...]

    @pl.when(pl.program_id(0) == 0)
    def _():
        m_ref[...] = jnp.zeros_like(m_ref)

    outs = []
    total = m_ref[...]
    for j in range(group):
        span = slice(j * width, (j + 1) * width)
        table = jnp.exp(jnp.minimum(log_col[0, :, j : j + 1] - log_row[0, j : j + 1, :], 0.0))
        e = e_ref[:, span]
        outs.append(dot_both(table * scores, e, COL_COL, split))
        inner = dot_exact_right(e, x_ref[:, span], ROW_ROW, split)
        total = total + table * inner * step_row[0, j : j + 1, :]
    g_ref[...] = jnp.concatenate(outs, axis=1)
    m_ref[...] = total


def exchange(decay, state, axis, reverse):
    count = lax.axis_size(axis)
    me = lax.axis_index(axis)
    rows = state.shape[0]
    before_decay, before = jnp.ones_like(decay), jnp.zeros_like(state)
    hop = 1
    while hop < count:
        sent = jnp.concatenate([state, jnp.broadcast_to(decay, (8, decay.shape[1]))], axis=0)
        got = lax.ppermute(sent, axis, [(i, i ^ hop) for i in range(count)])
        got_state, got_decay = got[:rows], got[rows : rows + 1]
        late = (lax.bitwise_and(me, hop) != 0) != reverse
        before = jnp.where(late, before + before_decay * got_state, before)
        before_decay = jnp.where(late, before_decay * got_decay, before_decay)
        state = jnp.where(late, state + decay * got_state, got_state + got_decay * state)
        decay = decay * got_decay
        hop *= 2
    return before


def on_device(
    inputs, gates, b_proj, c_proj, step_size, decay_rate, norm_gain, out_weight, grad_out
):
    length, width = inputs.shape
    heads = step_size.shape[0]
    head_width = width // heads
    states = b_proj.shape[1]
    group = 128 // head_width
    groups = heads // group
    lanes = group * head_width

    grad_full = lax.all_gather(grad_out, "head", axis=1, tiled=True)
    weight_full = lax.all_gather(out_weight, "seq", axis=0, tiled=True)
    grad_columns = lax.all_to_all(grad_full, "seq", split_axis=1, concat_axis=0, tiled=True)

    later = lax.broadcasted_iota(jnp.int32, (length, length), 0)
    earlier = lax.broadcasted_iota(jnp.int32, (length, length), 1)
    causal = (later >= earlier).astype(F32)
    logs = -dot_high(decay_rate[:, None] * step_size, causal, ROW_ROW)
    scores = dot_dims(c_proj, b_proj, ROW_ROW) * causal
    step_rows = step_size.reshape(groups, group, length)
    log_rows = logs.reshape(groups, group, length)
    step_cols = step_rows.transpose(0, 2, 1)
    log_cols = log_rows.transpose(0, 2, 1)

    row_spec = pl.BlockSpec((1, group, length), lambda i: (i, 0, 0))
    col_spec = pl.BlockSpec((1, length, group), lambda i: (i, 0, 0))
    wide_spec = pl.BlockSpec((length, lanes), lambda i: (0, i))
    square_spec = pl.BlockSpec((length, length), lambda i: (0, 0))
    key_spec = pl.BlockSpec((length, states), lambda i: (0, 0))
    state_spec = pl.BlockSpec((states, lanes), lambda i: (0, i))
    wide = jax.ShapeDtypeStruct((length, width), F32)

    def forward_body(*refs):
        forward_kernel(group, *refs)

    def backward_body(*refs):
        backward_kernel(group, *refs)

    flops = 8 * length * length * width
    y_local, front, tail, step, state_local = pl.pallas_call(
        forward_body,
        grid=(groups,),
        in_specs=[wide_spec, key_spec, square_spec, row_spec, row_spec, col_spec, col_spec],
        out_specs=[wide_spec] * 4 + [state_spec],
        out_shape=[wide] * 4 + [jax.ShapeDtypeStruct((states, width), F32)],
        cost_estimate=pl.CostEstimate(
            flops=flops, bytes_accessed=20 * length * width, transcendentals=heads * length * length
        ),
        name="span_forward",
    )(inputs, b_proj, scores, step_rows, log_rows, step_cols, log_cols)
    decay = front[length - 1 :, :]
    state_in = exchange(decay, state_local, "seq", False)

    grad_normed = jnp.dot(grad_full, weight_full, preferred_element_type=F32)
    y = y_local + front * dot_exact_left(c_proj, state_in, ROW_COL)
    gate_values = gates.astype(F32)
    sigmoid_gate = jax.nn.sigmoid(gate_values)
    gated = y * gate_values * sigmoid_gate
    total_width = width * lax.axis_size("head")
    scaled = grad_normed * norm_gain[None, :]
    sums = lax.psum(
        jnp.stack([jnp.sum(gated * gated, axis=1), jnp.sum(scaled * gated, axis=1)]), "head"
    )
    inv_rms = lax.rsqrt(sums[0] / total_width + EPSILON)
    scaled_back = (inv_rms * inv_rms * sums[1] / total_width)[:, None]
    inv_rms = inv_rms[:, None]
    normed = (gated * inv_rms * norm_gain[None, :]).astype(BF16)
    normed_full = lax.all_gather(normed, "seq", axis=0, tiled=True)
    gain_part = jnp.sum(grad_normed * gated * inv_rms, axis=0)
    grad_gated = inv_rms * (scaled - gated * scaled_back)
    grad_y = grad_gated * gate_values * sigmoid_gate
    grad_gates = (
        grad_gated * y * sigmoid_gate * (1.0 + gate_values * (1.0 - sigmoid_gate))
    ).astype(BF16)
    fronted = front * grad_y
    adjoint_local = dot_exact_left(c_proj, fronted, COL_COL)
    adjoint_in = exchange(decay, adjoint_local, "seq", True)

    g_local, mixed = pl.pallas_call(
        backward_body,
        grid=(groups,),
        in_specs=[wide_spec, wide_spec, square_spec, row_spec, row_spec, col_spec],
        out_specs=[wide_spec, square_spec],
        out_shape=[wide, jax.ShapeDtypeStruct((length, length), F32)],
        cost_estimate=pl.CostEstimate(
            flops=2 * flops,
            bytes_accessed=12 * length * width,
            transcendentals=heads * length * length,
        ),
        name="span_backward",
    )(inputs, grad_y, scores, step_rows, log_rows, log_cols)
    mixed = mixed * causal
    values = inputs.astype(F32)
    grad_c = dot_exact_right(mixed, b_proj, ROW_COL) + dot_both(fronted, state_in, ROW_ROW)
    g = g_local + tail * dot_exact_left(b_proj, adjoint_in, ROW_COL)
    grad_inputs = (step * g).astype(BF16)
    grad_b = dot_exact_right(mixed, c_proj, COL_COL) + dot_both(
        values * (step * tail), adjoint_in, ROW_ROW
    )
    owner = lax.broadcasted_iota(jnp.int32, (heads, width), 1) // head_width
    pick = (owner == lax.broadcasted_iota(jnp.int32, (heads, width), 0)).astype(BF16)
    q_terms = dot_exact_left(pick, g * values, ROW_ROW)
    row_part = dot_exact_left(pick, y * grad_y, ROW_ROW)
    state_end = decay * state_in + state_local
    boundary = jnp.sum(jnp.sum(adjoint_in * state_end, axis=0).reshape(heads, head_width), axis=1)
    log_grad = dot_high(row_part - step_size * q_terms, causal, ROW_COL) + boundary[:, None]
    grad_step = q_terms - decay_rate[:, None] * log_grad
    rate_part = -jnp.sum(step_size * log_grad, axis=1)
    both = lax.psum(jnp.concatenate([grad_b, grad_c], axis=1), "head")
    grad_b, grad_c = both[:, :states], both[:, states:]
    sums = lax.psum(jnp.concatenate([gain_part, rate_part]), "seq")
    grad_gain, grad_rate = sums[:width], sums[width:]
    grad_weight = lax.dot_general(
        grad_columns, normed_full, (COL_COL, ((), ())), preferred_element_type=F32
    )
    return (grad_inputs, grad_gates, grad_b, grad_c, grad_step, grad_rate, grad_gain, grad_weight)


def solution(mesh):
    in_specs = (
        P("seq", "head"),
        P("seq", "head"),
        P("seq", None),
        P("seq", None),
        P("head", "seq"),
        P("head"),
        P("head"),
        P("seq", "head"),
        P("seq", "head"),
    )
    out_specs = (
        P("seq", "head"),
        P("seq", "head"),
        P("seq", None),
        P("seq", None),
        P("head", "seq"),
        P("head"),
        P("head"),
        P("seq", "head"),
    )
    return jax.shard_map(
        on_device, mesh=mesh, in_specs=in_specs, out_specs=out_specs, check_vma=False
    )
```

time: 623 us -> 274 us (0.44); the launches traced: 613 us -> 272 us
  matrix products: 245 us -> 26.4 us
  other arithmetic: 118 us -> 13.2 us
  waiting for transfers between devices: 71.9 us -> 148 us
  local copies, waits for them, and re-layouts: 88.5 us -> 15.8 us
  blocking collectives: 51.5 us -> 24.2 us
  loops' own time: 22.8 us -> 0 us
  Pallas kernels: 0 us -> 17.6 us
  starting transfers between devices: 0.42 us -> 12.8 us
    dot_general x181 -> x25, matrix products: 245 us -> 26.4 us  [the longest x21 13.6 us: dot_dims(): lax.dot_general(left, right, (dims, ((), ())), preferred_element_type=F32)]
    ppermute x0 -> x6, waiting for transfers between devices: none -> 51.9 us  [exchange(): got = lax.ppermute(sent, axis, [(i, i ^ hop) for i in range(count)])]
    mul x48 -> x0, other arithmetic: 43.4 us -> none  [the longest x32 43.3 us: decay_table(): logs = -jnp.cumsum(rate * step)]
    reduce_sum x19 -> x2, other arithmetic: 34 us -> 1.62 us  [the longest x1 1.51 us: on_device(): jnp.sum(adjoint_in * state_end, axis=0).reshape(heads, head_width)]
    dynamic_slice x46 -> x0, local copies, waits for them, and re-layouts: 28.8 us -> none  [the longest x32 18.6 us: on_device(): head_out = lax.map(output_head, (step_size, decay_rate, values, state_in))]
    all_to_all x0 -> x1, waiting for transfers between devices: none -> 26.4 us  [on_device(): lax.all_to_all(grad_full, 'seq', split_axis=1, concat_axis=0, tiled=True)]
    another operation x4 -> x0, loops' own time: 22.8 us -> none  [the longest x1 22.3 us: on_device(): lax.map(backward_head, (step_size, decay_rate, values, grads, state_in, a...]
    dynamic_update_slice x32 -> x0, local copies, waits for them, and re-layouts: 22.7 us -> none  [on_device(): lax.map(backward_head, (step_size, decay_rate, values, grads, state_in, a...]
  transfers between devices with their start and end apart: 6 -> 11, of which waited for: 4 -> 8; matrix products, arithmetic and copies ran while one was open for 70% -> 9% of each run, Pallas kernels for 0% -> 6%
where the time goes in v1:
time: 274 us; the launch traced here: 272 us
  waiting for transfers between devices  148 us (54%)
  matrix products  26.4 us (10%)
  blocking collectives  24.2 us (9%)
  Pallas kernels  17.6 us (6%)
  local copies, waits for them, and re-layouts  15.8 us (6%)
  between operations  14.2 us (5%)
  other arithmetic  13.2 us (5%)
  starting transfers between devices  12.8 us (5%)
    all_gather x1, waiting for transfers between devices, on_device(): weight_full = lax.all_gather(out_weight, 'seq', axis=0, tiled=True)  53.3 us
    ppermute x6, waiting for transfers between devices, exchange(): got = lax.ppermute(sent, axis, [(i, i ^ hop) for i in range(count)])  51.9 us
    all_to_all x1, waiting for transfers between devices, on_device(): lax.all_to_all(grad_full, 'seq', split_axis=1, concat_axis=0, tiled=True)  26.4 us
    all_gather x1, waiting for transfers between devices, on_device(): normed_full = lax.all_gather(normed, 'seq', axis=0, tiled=True)  15.3 us
    dot_general x21, matrix products, dot_dims(): lax.dot_general(left, right, (dims, ((), ())), preferred_element_type=F32)  13.6 us
    psum x1, blocking collectives, on_device(): sums = lax.psum(jnp.concatenate([gain_part, rate_part]), 'seq')  12.5 us
    psum x1, blocking collectives, on_device(): lax.psum(jnp.stack([jnp.sum(gated * gated, axis=1), jnp.sum(scaled * gate...  11.7 us
    pallas_call x1, Pallas kernels, on_device(): pl.pallas_call(backward_body, grid=(groups,), in_specs=[wide_spec, wide_s...  9.14 us
  transfers between devices with their start and end apart: 11, of which 8 were waited for; matrix products, arithmetic and copies ran while one was open for 9% of the time, Pallas kernels for 6%

profile of v1, /device:TPU:0, one launch (start us, length us, event | category | flops | bytes accessed | tf_op | source)
XLA Modules:
  0.0 272.3 jit_solution(10289621390315950280)
XLA Ops:
  7.2 2.0 copy.51
  9.4 0.7 all-gather.6.cloned.1.call-update
  10.5 1.4 copy.47
  11.9 1.3 copy.48.refs_5_
  13.2 0.9 convolution_select_fusion.refs_2_
  14.1 8.4 %span_forward.1 = (f32[256,1024]{1,0:T(8,128)}, f32[256,1024]{1,0:T(8,128)}, f32[256,1024]{1,0:T(8,128)}, f32[256,1024]{1,0:T(8,128)}, f32[128,1024]{1,0:T(8,128)}) custom-call(bf16[256,1024]{1,0:T(8,128)(2,1)} %refs_0_.3, bf16[256,128]{1,0:T(8,128)(2,1)} %refs_1_.1, f32[256,256]{1,0:T(8,128)} %convolution_select_fusion.refs_2_, f32[8,2,256]{2,1,0:T(2,128)} %copy-done.16, ...), custom_call_target="tpu_custom_call" | custom-call | flops 536870912 | bytes 5242880 | tf_op jit(solution)/shard_map/span_forward/pallas_call | solution.py:163
  22.6 0.8 slice.51
  23.4 1.1 pad_maximum_fusion.1
  25.0 1.6 collective-permute-done
  26.6 0.8 fusion.70
  27.3 1.1 add_select_fusion.7
  28.5 3.0 %collective-permute-start.1 = (f32[136,1024]{1,0:T(8,128)S(1)}, f32[136,1024]{1,0:T(8,128)S(1)}, u32[]{:S(2)}, u32[]{:S(2)}) collective-permute-start(f32[136,1024]{1,0:T(8,128)S(1)} %pad_maximum_fusion.2), channel_id=1, source_target_pairs={{0,8},{4,12},{8,0},{12,4},{16,24},{20,28},{24,16},{28,20},{1,9},{5... | collective-permute-start | bytes 1671176 | tf_op jit(solution)/shard_map/ppermute | solution.py:112
  31.5 12.9 %collective-permute-done.1 = f32[136,1024]{1,0:T(8,128)S(1)} collective-permute-done((f32[136,1024]{1,0:T(8,128)S(1)}, f32[136,1024]{1,0:T(8,128)S(1)}, u32[]{:S(2)}, u32[]{:S(2)}) %collective-permute-start.1) | collective-permute-done | bytes 557088 | tf_op jit(solution)/shard_map/ppermute | solution.py:112
  44.6 1.8 collective-permute-start.2
  46.4 12.4 %collective-permute-done.2 = f32[136,1024]{1,0:T(8,128)S(1)} collective-permute-done((f32[136,1024]{1,0:T(8,128)S(1)}, f32[136,1024]{1,0:T(8,128)S(1)}, u32[]{:S(2)}, u32[]{:S(2)}) %collective-permute-start.2) | collective-permute-done | bytes 557088 | tf_op jit(solution)/shard_map/ppermute | solution.py:112
  59.0 1.3 fusion.66
  60.3 53.3 %all-gather.6.cloned.1.call-done = bf16[4096,1024]{1,0:T(8,128)(2,1)} async-done(((bf16[512,1024]{1,0:T(8,128)(2,1)}), bf16[4096,1024]{1,0:T(8,128)(2,1)}) %all-gather.6.cloned.1.call-update) | async-done | bytes 8388624 | tf_op jit(solution)/shard_map/all_gather | solution.py:135
  113.6 6.5 %fusion.72 = f32[256,1024]{1,0:T(8,128)S(1)} fusion(bf16[256,4096]{0,1:T(8,128)(2,1)} %all-gather.4.cloned.1.call-done, bf16[4096,1024]{1,0:T(8,128)(2,1)} %all-gather.6.cloned.1.call-done), kind=kOutput, calls=%fused_computation.141 | convolution fusion | flops 2147483648 | bytes 11534336 | tf_op jit(solution)/shard_map/dot_general | solution.py:177
  120.1 2.4 multiply_reduce_fusion.2
  122.5 11.7 %psum.21 = f32[2,256]{1,0:T(2,128)S(1)} all-reduce(f32[2,256]{1,0:T(2,128)S(1)} %pad_maximum_fusion.8), channel_id=1, replica_groups=mesh['seq'=8,'head'=4] {'head'}, use_global_device_ids=true, to_apply=%region_2.3 | all-reduce | flops 512 | bytes 4096 | tf_op jit(solution)/shard_map/psum | solution.py:184
  134.2 3.5 %fusion.10 = (bf16[256,1024]{1,0:T(8,128)(2,1)S(1)}, f32[256,1024]{1,0:T(8,128)S(1)}, bf16[256,1024]{1,0:T(8,128)(2,1)}, f32[1024]{0:T(1024)S(1)}, bf16[256,1024]{1,0:T(8,128)(2,1)}) fusion(f32[256,1024]{1,0:T(8,128)S(1)} %copy-done.5, f32[256]{0:T(256)S(1)} %multiply_multiply_fusion, f32[256,1024]{1,0:T(8,128)S(1)} %get-tuple-element.83, ...), kind=kLoop, calls=%fused_computation.39 | loop fusion | flops 7601152 | bytes 6301696 | tf_op jit(solution)/shard_map/convert_element_type | solution.py:20
  138.7 0.9 pad_maximum_fusion
  139.6 9.1 %span_backward.1 = (f32[256,1024]{1,0:T(8,128)}, f32[256,256]{1,0:T(8,128)}) custom-call(bf16[256,1024]{1,0:T(8,128)(2,1)} %refs_0_.3, f32[256,1024]{1,0:T(8,128)} %copy-done.1, f32[256,256]{1,0:T(8,128)} %convolution_select_fusion.refs_2_, f32[8,2,256]{2,1,0:T(2,128)} %copy-done.16, f32[8,2,256]{2,1,0:T(2,128)} %copy-done.17, f32[8,256,2]{2,1,0:T(8,128)} %bitcast.62), custom_call_target="tpu_custom_call" | custom-call | flops 1073741824 | bytes 3145728 | tf_op jit(solution)/shard_map/span_backward/pallas_call | solution.py:202
  148.7 1.2 fusion.50
  150.0 0.8 fusion.69
  150.7 1.1 add_select_fusion.5
  151.9 1.5 collective-permute-start.4
  154.3 12.8 %collective-permute-done.4 = f32[136,1024]{1,0:T(8,128)S(1)} collective-permute-done((f32[136,1024]{1,0:T(8,128)S(1)}, f32[136,1024]{1,0:T(8,128)S(1)}, u32[]{:S(2)}, u32[]{:S(2)}) %collective-permute-start.4) | collective-permute-done | bytes 557088 | tf_op jit(solution)/shard_map/ppermute | solution.py:112
  167.0 0.8 broadcast_select_fusion
  168.0 1.2 collective-permute-start.5
  170.1 12.2 %collective-permute-done.5 = f32[136,1024]{1,0:T(8,128)S(1)} collective-permute-done((f32[136,1024]{1,0:T(8,128)S(1)}, f32[136,1024]{1,0:T(8,128)S(1)}, u32[]{:S(2)}, u32[]{:S(2)}) %collective-permute-start.5) | collective-permute-done | bytes 557088 | tf_op jit(solution)/shard_map/ppermute | solution.py:112
  182.2 1.5 multiply_reduce_fusion.3
  184.4 1.3 convert_multiply_fusion.4
  186.6 0.7 pad_maximum_fusion.6
  188.0 4.5 %all-to-all-start = ((bf16[256,8,512]{0,2,1:T(8,128)(2,1)}), bf16[256,8,512]{0,2,1:T(8,128)(2,1)}, u32[]{:S(2)}, u32[]{:S(2)}) async-start(bf16[256,8,512]{0,2,1:T(8,128)(2,1)} %bitcast.22), calls=%async_computation | async-start | bytes 4194304 | tf_op jit(solution)/shard_map/all_to_all | solution.py:136
  192.5 26.4 %all-to-all-done = bf16[256,8,512]{0,2,1:T(8,128)(2,1)} async-done(((bf16[256,8,512]{0,2,1:T(8,128)(2,1)}), bf16[256,8,512]{0,2,1:T(8,128)(2,1)}, u32[]{:S(2)}, u32[]{:S(2)}) %all-to-all-start) | async-done | bytes 2097184 | tf_op jit(solution)/shard_map/all_to_all | solution.py:136
  219.0 4.0 %copy.54 = bf16[8,256,512]{2,1,0:T(8,128)(2,1)} copy(bf16[8,256,512]{1,2,0:T(8,128)(2,1)} %bitcast.23) | data formatting | bytes 4194304 | tf_op jit(solution)/shard_map/all_to_all | solution.py:136
  223.4 1.3 fusion.27
  224.7 1.3 convolution_add_fusion.11
  226.3 0.9 multiply_reduce_fusion.4
  227.2 12.5 %psum.23 = f32[1040]{0:T(1024)S(1)} all-reduce(f32[1040]{0:T(1024)S(1)} %pad_maximum_fusion.7), channel_id=1, replica_groups=mesh['seq'=8,'head'=4] {'seq'}, use_global_device_ids=true, to_apply=%region_8.9 | all-reduce | flops 1040 | bytes 8320 | tf_op jit(solution)/shard_map/psum | solution.py:234
  240.3 0.6 slice.83
  240.9 1.0 fusion.71
  241.9 0.8 copy.56
  242.6 0.8 copy.55
  243.4 15.3 %all-gather.8.cloned.1.call-done = bf16[2048,1024]{1,0:T(8,128)(2,1)} async-done(((bf16[256,1024]{1,0:T(8,128)(2,1)}), bf16[2048,1024]{1,0:T(8,128)(2,1)}) %all-gather.8.cloned.1.call-update) | async-done | bytes 4194320 | tf_op jit(solution)/shard_map/all_gather | solution.py:191
  258.7 5.2 %convolution_bitcast_fusion = f32[512,1024]{0,1:T(8,128)S(1)} fusion(bf16[2048,1024]{1,0:T(8,128)(2,1)} %all-gather.8.cloned.1.call-done, bf16[2048,512]{1,0:T(8,128)(2,1)} %bitcast.60), kind=kOutput, calls=%fused_computation.4 | convolution fusion | flops 2147483648 | bytes 8388608 | tf_op jit(solution)/shard_map/dot_general | solution.py:236
  263.9 1.8 copy.57
  (96 shorter events, 7.6 us)
Async XLA Ops:
  7.2 6.1 %copy-start = (bf16[256,128]{1,0:T(8,128)(2,1)S(1)}, bf16[256,128]{1,0:T(8,128)(2,1)}, u32[]{:S(2)}) copy-start(bf16[256,128]{1,0:T(8,128)(2,1)} %param.12) | copy-start | bytes 196612
  7.2 2.9 %copy-start.18 = (f32[16,256]{1,0:T(8,128)S(1)}, f32[16,256]{1,0:T(8,128)}, u32[]{:S(2)}) copy-start(f32[16,256]{1,0:T(8,128)} %param.13) | copy-start | bytes 49156
  7.2 3.0 %copy-start.20 = (f32[16]{0:T(128)S(1)}, f32[16]{0:T(128)}, u32[]{:S(2)}) copy-start(f32[16]{0:T(128)} %param.14) | copy-start | bytes 196
  7.2 53.1 %all-gather.4.cloned.1.call-start = ((), (), s32[]{:S(2)}) async-start(), calls=%async_computation.1 | async-start | bytes 2621440 | tf_op jit(solution)/shard_map/all_gather | solution.py:134
  9.3 3.9 %copy-start.9 = (bf16[256,128]{1,0:T(8,128)(2,1)S(1)}, bf16[256,128]{1,0:T(8,128)(2,1)}, u32[]{:S(2)}) copy-start(bf16[256,128]{1,0:T(8,128)(2,1)} %refs_1_.1) | copy-start | bytes 196612
  9.3 104.2 %all-gather.6.cloned.1.call-start = ((), (), s32[]{:S(2)}) async-start(), calls=%async_computation.2 | async-start | bytes 9437184 | tf_op jit(solution)/shard_map/all_gather | solution.py:135
  10.1 230.8 %all-reduce.2.cloned.1.call-start = ((), (), s32[]{:S(2)}) async-start(), calls=%async_computation.3 | async-start | bytes 524288 | tf_op jit(solution)/shard_map/psum | solution.py:232
  10.2 4.0 %copy-start.16 = (f32[8,2,256]{2,1,0:T(2,128)}, f32[8,2,256]{2,1,0:T(2,128)S(1)}, u32[]{:S(2)}) copy-start(f32[8,2,256]{2,1,0:T(2,128)S(1)} %reshape.53.refs_3_) | copy-start | bytes 49156
  10.5 3.7 %copy-start.17 = (f32[8,2,256]{2,1,0:T(2,128)}, f32[8,2,256]{2,1,0:T(2,128)S(1)}, u32[]{:S(2)}) copy-start(f32[8,2,256]{2,1,0:T(2,128)S(1)} %reshape.54.refs_4_) | copy-start | bytes 49156
  24.4 2.1 collective-permute-start
  28.5 15.9 %collective-permute-start.1 = (f32[136,1024]{1,0:T(8,128)S(1)}, f32[136,1024]{1,0:T(8,128)S(1)}, u32[]{:S(2)}, u32[]{:S(2)}) collective-permute-start(f32[136,1024]{1,0:T(8,128)S(1)} %pad_maximum_fusion.2), channel_id=1, source_target_pairs={{0,8},{4,12},{8,0},{12,4},{16,24},{20,28},{24,16},{28,20},{1,9},{5... | collective-permute-start | bytes 1671176 | tf_op jit(solution)/shard_map/ppermute | solution.py:112
  44.6 14.3 %collective-permute-start.2 = (f32[136,1024]{1,0:T(8,128)S(1)}, f32[136,1024]{1,0:T(8,128)S(1)}, u32[]{:S(2)}, u32[]{:S(2)}) collective-permute-start(f32[136,1024]{1,0:T(8,128)S(1)} %pad_maximum_fusion.3), channel_id=1, source_target_pairs={{0,16},{4,20},{8,24},{12,28},{16,0},{20,4},{24,8},{28,12},{1,17},{... | collective-permute-start | bytes 1671176 | tf_op jit(solution)/shard_map/ppermute | solution.py:112
  60.3 59.7 %copy-start.5 = (f32[256,1024]{1,0:T(8,128)S(1)}, f32[256,1024]{1,0:T(8,128)}, u32[]{:S(2)}) copy-start(f32[256,1024]{1,0:T(8,128)} %get-tuple-element.17) | copy-start | bytes 3145732
  60.3 59.7 %copy-start.15 = (bf16[256,1024]{1,0:T(8,128)(2,1)S(1)}, bf16[256,1024]{1,0:T(8,128)(2,1)}, u32[]{:S(2)}) copy-start(bf16[256,1024]{1,0:T(8,128)(2,1)} %param.10) | copy-start | bytes 1572868
  60.3 59.7 %copy-start.19 = (f32[1024]{0:T(1024)S(1)}, f32[1024]{0:T(1024)}, u32[]{:S(2)}) copy-start(f32[1024]{0:T(1024)} %param.15) | copy-start | bytes 12292
  113.6 6.5 %copy-start.14 = (f32[1024,256]{0,1:T(8,128)S(1)}, f32[1024,256]{0,1:T(8,128)}, u32[]{:S(2)}) copy-start(f32[1024,256]{0,1:T(8,128)} %fusion.66) | copy-start | bytes 3145732
  120.0 2.4 copy-start.8
  134.2 3.6 %copy-start.6 = (f32[256,1024]{1,0:T(8,128)S(1)}, f32[256,1024]{1,0:T(8,128)}, u32[]{:S(2)}) copy-start(f32[256,1024]{1,0:T(8,128)} %get-tuple-element.17) | copy-start | bytes 3145732
  137.7 1.0 copy-start.1
  139.6 9.2 %copy-start.10 = (bf16[256,128]{1,0:T(8,128)(2,1)S(1)}, bf16[256,128]{1,0:T(8,128)(2,1)}, u32[]{:S(2)}) copy-start(bf16[256,128]{1,0:T(8,128)(2,1)} %refs_1_.1) | copy-start | bytes 196612
  139.6 10.4 %collective-permute-start.3 = (f32[136,1024]{1,0:T(8,128)}, f32[136,1024]{1,0:T(8,128)}, u32[]{:S(2)}, u32[]{:S(2)}) collective-permute-start(f32[136,1024]{1,0:T(8,128)} %pad_maximum_fusion), channel_id=1, source_target_pairs={{0,4},{4,0},{8,12},{12,8},{16,20},{20,16},{24,28},{28,24},{1,5},{5... | collective-permute-start | bytes 1671176 | tf_op jit(solution)/shard_map/ppermute | solution.py:112
  148.7 4.8 %copy-start.7 = (f32[256,256]{1,0:T(8,128)S(1)}, f32[256,256]{1,0:T(8,128)}, u32[]{:S(2)}) copy-start(f32[256,256]{1,0:T(8,128)} %get-tuple-element.21) | copy-start | bytes 786436
  151.9 15.1 %collective-permute-start.4 = (f32[136,1024]{1,0:T(8,128)S(1)}, f32[136,1024]{1,0:T(8,128)S(1)}, u32[]{:S(2)}, u32[]{:S(2)}) collective-permute-start(f32[136,1024]{1,0:T(8,128)S(1)} %pad_maximum_fusion.4), channel_id=1, source_target_pairs={{0,8},{4,12},{8,0},{12,4},{16,24},{20,28},{24,16},{28,20},{1,9},{5... | collective-permute-start | bytes 1671176 | tf_op jit(solution)/shard_map/ppermute | solution.py:112
  167.9 14.3 %copy-start.4 = (f32[128,1024]{1,0:T(8,128)S(1)}, f32[128,1024]{1,0:T(8,128)}, u32[]{:S(2)}) copy-start(f32[128,1024]{1,0:T(8,128)} %get-tuple-element.18) | copy-start | bytes 1572868
  168.0 14.2 %collective-permute-start.5 = (f32[136,1024]{1,0:T(8,128)S(1)}, f32[136,1024]{1,0:T(8,128)S(1)}, u32[]{:S(2)}, u32[]{:S(2)}) collective-permute-start(f32[136,1024]{1,0:T(8,128)S(1)} %pad_maximum_fusion.5), channel_id=1, source_target_pairs={{0,16},{4,20},{8,24},{12,28},{16,0},{20,4},{24,8},{28,12},{1,17},{... | collective-permute-start | bytes 1671176 | tf_op jit(solution)/shard_map/ppermute | solution.py:112
  182.2 1.8 copy-start.3
  182.2 1.8 copy-start.11
  182.2 1.9 copy-start.12
  182.2 2.2 copy-start.13
  187.4 71.3 %all-gather.8.cloned.1.call-start = ((), (), s32[]{:S(2)}) async-start(), calls=%async_computation.4 | async-start | bytes 4718592 | tf_op jit(solution)/shard_map/all_gather | solution.py:191
  188.0 31.0 %all-to-all-start = ((bf16[256,8,512]{0,2,1:T(8,128)(2,1)}), bf16[256,8,512]{0,2,1:T(8,128)(2,1)}, u32[]{:S(2)}, u32[]{:S(2)}) async-start(bf16[256,8,512]{0,2,1:T(8,128)(2,1)} %bitcast.22), calls=%async_computation | async-start | bytes 4194304 | tf_op jit(solution)/shard_map/all_to_all | solution.py:136
  219.0 4.0 %copy-start.2 = (f32[256,1024]{1,0:T(8,128)S(1)}, f32[256,1024]{1,0:T(8,128)}, u32[]{:S(2)}) copy-start(f32[256,1024]{1,0:T(8,128)} %copy-done.1) | copy-start | bytes 3145732
Sparse Core Ops, SparseCore 0:
  10.2 48.3 all-gather.3
  60.5 53.0 all-gather.5
  187.5 32.8 all-reduce.1
  222.1 36.5 all-gather.7

commit v2 on v1

--- a/solution.py
+++ b/solution.py
@@ -120,6 +120,21 @@
     return before
 
 
+def gather_columns(block, axis):
+    count = lax.axis_size(axis)
+    me = lax.axis_index(axis)
+    blocks = [block] + [
+        lax.ppermute(block, axis, [((i + ahead) % count, i) for i in range(count)])
+        for ahead in range(1, count)
+    ]
+    stacked = jnp.stack(blocks)
+    ordered = [
+        lax.dynamic_index_in_dim(stacked, lax.rem(j - me + count, count), 0, False)
+        for j in range(count)
+    ]
+    return jnp.concatenate(ordered, axis=1)
+
+
 def on_device(
     inputs, gates, b_proj, c_proj, step_size, decay_rate, norm_gain, out_weight, grad_out
 ):
@@ -131,9 +146,10 @@
     groups = heads // group
     lanes = group * head_width
 
-    grad_full = lax.all_gather(grad_out, "head", axis=1, tiled=True)
     weight_full = lax.all_gather(out_weight, "seq", axis=0, tiled=True)
+    grad_full = gather_columns(grad_out, "head")
     grad_columns = lax.all_to_all(grad_full, "seq", split_axis=1, concat_axis=0, tiled=True)
+    grad_full, grad_columns = lax.optimization_barrier((grad_full, grad_columns))
 
     later = lax.broadcasted_iota(jnp.int32, (length, length), 0)
     earlier = lax.broadcasted_iota(jnp.int32, (length, length), 1)
@@ -229,7 +245,10 @@
     log_grad = dot_high(row_part - step_size * q_terms, causal, ROW_COL) + boundary[:, None]
     grad_step = q_terms - decay_rate[:, None] * log_grad
     rate_part = -jnp.sum(step_size * log_grad, axis=1)
-    both = lax.psum(jnp.concatenate([grad_b, grad_c], axis=1), "head")
+    both, normed_full, rate_part = lax.optimization_barrier(
+        (jnp.concatenate([grad_b, grad_c], axis=1), normed_full, rate_part)
+    )
+    both = lax.psum(both, "head")
     grad_b, grad_c = both[:, :states], both[:, states:]
     sums = lax.psum(jnp.concatenate([gain_part, rate_part]), "seq")
     grad_gain, grad_rate = sums[:width], sums[width:]

time: 274 us -> 262 us (0.956)
  waiting for transfers between devices: 148 us -> 112 us
  other arithmetic: 13.2 us -> 23.4 us
  blocking collectives: 24.2 us -> 33.2 us
  starting transfers between devices: 12.8 us -> 17.1 us
    all_gather x1, waiting for transfers between devices: 53.3 us -> 0.01 us  [on_device(): weight_full = lax.all_gather(out_weight, 'seq', axis=0, tiled=True)]
    ppermute x0 -> x3, waiting for transfers between devices: none -> 30.1 us  [gather_columns(): lax.ppermute(block, axis, [((i + ahead) % count, i) for i in range(count)])]
    all_to_all x1, waiting for transfers between devices: 26.4 us -> 0.01 us  [on_device(): lax.all_to_all(grad_full, 'seq', split_axis=1, concat_axis=0, tiled=True)]
    ppermute x6, waiting for transfers between devices: 51.9 us -> 67.9 us  [exchange(): got = lax.ppermute(sent, axis, [(i, i ^ hop) for i in range(count)])]
    all_gather x1, waiting for transfers between devices: 15.3 us -> 0.01 us  [on_device(): normed_full = lax.all_gather(normed, 'seq', axis=0, tiled=True)]
    psum x1, waiting for transfers between devices: 0.01 us -> 13.6 us  [on_device(): both = lax.psum(both, 'head')]
    psum x1, blocking collectives: 11.7 us -> 21 us  [on_device(): lax.psum(jnp.stack([jnp.sum(gated * gated, axis=1), jnp.sum(scaled * gate...]
    ppermute x0 -> x3, starting transfers between devices: none -> 6.58 us  [gather_columns(): lax.ppermute(block, axis, [((i + ahead) % count, i) for i in range(count)])]
  transfers between devices with their start and end apart: 11 -> 13, of which waited for: 8 -> 6; matrix products, arithmetic and copies ran while one was open for 9% -> 19% of each run, Pallas kernels for 6% -> 7%
where the time goes in v2:
time: 262 us; the launch traced here: 260 us
  waiting for transfers between devices  112 us (43%)
  blocking collectives  33.2 us (13%)
  matrix products  27.9 us (11%)
  other arithmetic  23.4 us (9%)
  Pallas kernels  17.8 us (7%)
  starting transfers between devices  17.1 us (7%)
  between operations  14.3 us (5%)
  local copies, waits for them, and re-layouts  13.8 us (5%)
    ppermute x6, waiting for transfers between devices, exchange(): got = lax.ppermute(sent, axis, [(i, i ^ hop) for i in range(count)])  67.9 us
    ppermute x3, waiting for transfers between devices, gather_columns(): lax.ppermute(block, axis, [((i + ahead) % count, i) for i in range(count)])  30.1 us
    psum x1, blocking collectives, on_device(): lax.psum(jnp.stack([jnp.sum(gated * gated, axis=1), jnp.sum(scaled * gate...  21 us
    dot_general x21, matrix products, dot_dims(): lax.dot_general(left, right, (dims, ((), ())), preferred_element_type=F32)  14.3 us
    psum x1, waiting for transfers between devices, on_device(): both = lax.psum(both, 'head')  13.6 us
    psum x1, blocking collectives, on_device(): sums = lax.psum(jnp.concatenate([gain_part, rate_part]), 'seq')  12.2 us
    pallas_call x1, Pallas kernels, on_device(): pl.pallas_call(backward_body, grid=(groups,), in_specs=[wide_spec, wide_s...  9.25 us
    pallas_call x1, Pallas kernels, on_device(): pl.pallas_call(forward_body, grid=(groups,), in_specs=[wide_spec, key_spe...  8.54 us
  transfers between devices with their start and end apart: 13, of which 6 were waited for; matrix products, arithmetic and copies ran while one was open for 19% of the time, Pallas kernels for 7%

profile of v2, /device:TPU:0, one launch (start us, length us, event | category | flops | bytes accessed | tf_op | source)
XLA Modules:
  0.0 259.9 jit_solution(10061078434152660753)
XLA Ops:
  8.7 0.9 convolution_negate_fusion
  9.7 1.3 copy.47
  11.0 1.3 copy.48.refs_5_
  12.4 0.9 convolution_select_fusion.refs_2_
  13.3 8.5 %span_forward.1 = (f32[256,1024]{1,0:T(8,128)}, f32[256,1024]{1,0:T(8,128)}, f32[256,1024]{1,0:T(8,128)}, f32[256,1024]{1,0:T(8,128)}, f32[128,1024]{1,0:T(8,128)}) custom-call(bf16[256,1024]{1,0:T(8,128)(2,1)} %refs_0_.3, bf16[256,128]{1,0:T(8,128)(2,1)} %refs_1_.1, f32[256,256]{1,0:T(8,128)} %convolution_select_fusion.refs_2_, f32[8,2,256]{2,1,0:T(2,128)} %copy-done.22, ...), custom_call_target="tpu_custom_call" | custom-call | flops 536870912 | bytes 5242880 | tf_op jit(solution)/shard_map/span_forward/pallas_call | solution.py:179
  21.9 0.8 slice.51
  22.7 1.1 pad_maximum_fusion.4
  24.6 2.6 %collective-permute-start.5 = (bf16[256,1024]{0,1:T(8,128)(2,1)S(1)}, bf16[256,1024]{0,1:T(8,128)(2,1)S(1)}, u32[]{:S(2)}, u32[]{:S(2)}) collective-permute-start(bf16[256,1024]{0,1:T(8,128)(2,1)S(1)} %copy.51), channel_id=1, source_target_pairs={{3,0},{0,1},{1,2},{2,3},{7,4},{4,5},{5,6},{6,7},{11,8},{8,9},{9,10... | collective-permute-start | bytes 1572872 | tf_op jit(solution)/shard_map/ppermute | solution.py:127
  27.2 2.6 collective-permute-start.4
  29.8 1.3 collective-permute-start.3
  32.0 0.9 pad_maximum_fusion.5
  32.9 1.5 collective-permute-start.1
  34.4 7.8 %collective-permute-done.5 = bf16[256,1024]{0,1:T(8,128)(2,1)S(1)} collective-permute-done((bf16[256,1024]{0,1:T(8,128)(2,1)S(1)}, bf16[256,1024]{0,1:T(8,128)(2,1)S(1)}, u32[]{:S(2)}, u32[]{:S(2)}) %collective-permute-start.5) | collective-permute-done | bytes 524320 | tf_op jit(solution)/shard_map/ppermute | solution.py:127
  42.1 22.3 %collective-permute-done.4 = bf16[256,1024]{0,1:T(8,128)(2,1)} collective-permute-done((bf16[256,1024]{0,1:T(8,128)(2,1)S(1)}, bf16[256,1024]{0,1:T(8,128)(2,1)}, u32[]{:S(2)}, u32[]{:S(2)}) %collective-permute-start.4) | collective-permute-done | bytes 524320 | tf_op jit(solution)/shard_map/ppermute | solution.py:127
  64.5 1.6 pad_maximum_fusion
  66.2 1.6 pad_maximum_fusion.2
  67.9 4.4 %all-to-all-start = ((bf16[256,8,512]{0,2,1:T(8,128)(2,1)}), bf16[256,8,512]{0,2,1:T(8,128)(2,1)}, u32[]{:S(2)}, u32[]{:S(2)}) async-start(bf16[256,8,512]{0,2,1:T(8,128)(2,1)} %pad_maximum_fusion.2), calls=%async_computation | async-start | bytes 4194304 | tf_op jit(solution)/shard_map/all_to_all | solution.py:151
  73.1 1.1 add_select_fusion.6
  74.3 0.9 pad_maximum_fusion.6
  75.2 1.9 collective-permute-start.2
  77.0 1.4 pad_maximum_fusion.1
  78.4 31.4 %collective-permute-done.2 = f32[136,1024]{1,0:T(8,128)} collective-permute-done((f32[136,1024]{1,0:T(8,128)}, f32[136,1024]{1,0:T(8,128)}, u32[]{:S(2)}, u32[]{:S(2)}) %collective-permute-start.2) | collective-permute-done | bytes 557088 | tf_op jit(solution)/shard_map/ppermute | solution.py:112
  109.9 1.4 add_select_fusion.2
  111.2 1.3 fusion.66
  112.5 3.9 %copy.55 = bf16[8,256,512]{2,1,0:T(8,128)(2,1)} copy(bf16[8,256,512]{1,2,0:T(8,128)(2,1)} %bitcast.23) | data formatting | bytes 4194304 | tf_op jit(solution)/shard_map/all_to_all | solution.py:151
  116.4 5.9 %fusion.72 = f32[256,1024]{1,0:T(8,128)S(1)} fusion(bf16[256,4096]{0,1:T(8,128)(2,1)S(1)} %pad_maximum_fusion.1, bf16[4096,1024]{1,0:T(8,128)(2,1)} %all-gather.3.cloned.1.call-done), kind=kOutput, calls=%fused_computation.147 | convolution fusion | flops 2147483648 | bytes 11534336 | tf_op jit(solution)/shard_map/dot_general | solution.py:193
  122.4 0.8 multiply_reduce_fusion.2
  123.3 21.0 %psum.21 = f32[2,256]{1,0:T(2,128)S(1)} all-reduce(f32[2,256]{1,0:T(2,128)S(1)} %pad_maximum_fusion.11), channel_id=1, replica_groups=mesh['seq'=8,'head'=4] {'head'}, use_global_device_ids=true, to_apply=%region_2.3 | all-reduce | flops 512 | bytes 4096 | tf_op jit(solution)/shard_map/psum | solution.py:200
  144.4 4.4 %fusion.10 = (bf16[256,1024]{1,0:T(8,128)(2,1)}, f32[256,1024]{1,0:T(8,128)S(1)}, bf16[256,1024]{1,0:T(8,128)(2,1)}, f32[1024]{0:T(1024)}, bf16[256,1024]{1,0:T(8,128)(2,1)}) fusion(f32[256,1024]{1,0:T(8,128)} %get-tuple-element.22, f32[256]{0:T(256)S(1)} %multiply_multiply_fusion, f32[256,1024]{1,0:T(8,128)S(1)} %get-tuple-element.97, ...), kind=kLoop, calls=%fused_computation.41 | loop fusion | flops 7601152 | bytes 6301696 | tf_op jit(solution)/shard_map/convert_element_type | solution.py:20
  149.1 1.4 reduce-precision_convert_fusion.3
  150.8 1.3 fusion.6
  152.1 0.8 pad_maximum_fusion.3
  153.0 9.2 %span_backward.1 = (f32[256,1024]{1,0:T(8,128)}, f32[256,256]{1,0:T(8,128)}) custom-call(bf16[256,1024]{1,0:T(8,128)(2,1)} %refs_0_.3, f32[256,1024]{1,0:T(8,128)} %copy-done.1, f32[256,256]{1,0:T(8,128)} %convolution_select_fusion.refs_2_, f32[8,2,256]{2,1,0:T(2,128)} %copy-done.22, f32[8,2,256]{2,1,0:T(2,128)} %copy-done.23, f32[8,256,2]{2,1,0:T(8,128)} %bitcast.78), custom_call_target="tpu_custom_call" | custom-call | flops 1073741824 | bytes 3145728 | tf_op jit(solution)/shard_map/span_backward/pallas_call | solution.py:218
  162.2 1.2 fusion.50
  163.5 1.2 convolution_add_fusion.7
  165.4 1.1 add_select_fusion.5
  166.6 1.5 collective-permute-start.7
  169.0 23.9 %collective-permute-done.7 = f32[136,1024]{1,0:T(8,128)S(1)} collective-permute-done((f32[136,1024]{1,0:T(8,128)S(1)}, f32[136,1024]{1,0:T(8,128)S(1)}, u32[]{:S(2)}, u32[]{:S(2)}) %collective-permute-start.7) | collective-permute-done | bytes 557088 | tf_op jit(solution)/shard_map/ppermute | solution.py:112
  194.9 0.9 fusion.27
  195.8 12.6 %collective-permute-done.8 = f32[136,1024]{1,0:T(8,128)S(1)} collective-permute-done((f32[136,1024]{1,0:T(8,128)S(1)}, f32[136,1024]{1,0:T(8,128)S(1)}, u32[]{:S(2)}, u32[]{:S(2)}) %collective-permute-start.8) | collective-permute-done | bytes 557088 | tf_op jit(solution)/shard_map/ppermute | solution.py:112
  208.4 1.3 multiply_reduce_fusion.3
  210.2 0.9 copy-done.17
  211.2 3.1 %convert_multiply_fusion.4 = (f32[256,1024]{1,0:T(8,128)S(1)}, bf16[256,1024]{1,0:T(8,128)(2,1)}, f32[256,1024]{1,0:T(8,128)S(1)}) fusion(bf16[256,1024]{1,0:T(8,128)(2,1)} %refs_0_.3, f32[256,1024]{1,0:T(8,128)} %get-tuple-element.20, f32[256,1024]{1,0:T(8,128)S(1)} %copy-done.17, f32[256,1024]{1,0:T(8,128)} %get-tuple-element.25, ...), kind=kOutput, calls=%fused_computation.24 | convolution fusion | flops 69599232 | bytes 7929856 | tf_op jit(solution)/shard_map/dot_general | solution.py:24
  215.2 0.9 multiply_subtract_fusion
  218.1 5.9 %fusion.74 = f32[512,1024]{1,0:T(8,128)} fusion(bf16[2048,512]{1,0:T(8,128)(2,1)S(1)} %bitcast.79, bf16[2048,1024]{1,0:T(8,128)(2,1)} %all-gather.5.cloned.1.call-done), kind=kOutput, calls=%fused_computation.149 | convolution fusion | flops 2147483648 | bytes 8388608 | tf_op jit(solution)/shard_map/dot_general | solution.py:255
  224.0 12.2 %psum.23 = f32[1040]{0:T(1024)S(1)} all-reduce(f32[1040]{0:T(1024)S(1)} %pad_maximum_fusion.10), channel_id=1, replica_groups=mesh['seq'=8,'head'=4] {'seq'}, use_global_device_ids=true, to_apply=%region_8.9 | all-reduce | flops 1040 | bytes 8320 | tf_op jit(solution)/shard_map/psum | solution.py:253
  237.2 13.6 %all-reduce.2.cloned.1.call-done = f32[256,256]{0,1:T(8,128)} async-done(((f32[256,256]{0,1:T(8,128)}), f32[256,256]{0,1:T(8,128)}) %all-reduce.2.cloned.1.call-update) | async-done | bytes 262160 | tf_op jit(solution)/shard_map/psum | solution.py:251
  250.9 1.0 fusion.71
  (123 shorter events, 14.5 us)
Async XLA Ops:
  7.2 5.2 %copy-start = (bf16[256,128]{1,0:T(8,128)(2,1)S(1)}, bf16[256,128]{1,0:T(8,128)(2,1)}, u32[]{:S(2)}) copy-start(bf16[256,128]{1,0:T(8,128)(2,1)} %param.12) | copy-start | bytes 196612
  7.2 5.2 %copy-start.12 = (bf16[256,128]{1,0:T(8,128)(2,1)S(1)}, bf16[256,128]{1,0:T(8,128)(2,1)}, u32[]{:S(2)}) copy-start(bf16[256,128]{1,0:T(8,128)(2,1)} %refs_1_.1) | copy-start | bytes 196612
  7.2 109.2 %all-gather.3.cloned.1.call-start = ((), (), s32[]{:S(2)}) async-start(), calls=%async_computation.1 | async-start | bytes 9437184 | tf_op jit(solution)/shard_map/all_gather | solution.py:149
  8.7 4.6 %copy-start.22 = (f32[8,2,256]{2,1,0:T(2,128)}, f32[8,2,256]{2,1,0:T(2,128)S(1)}, u32[]{:S(2)}) copy-start(f32[8,2,256]{2,1,0:T(2,128)S(1)} %reshape.61.refs_3_) | copy-start | bytes 49156
  9.7 3.6 %copy-start.23 = (f32[8,2,256]{2,1,0:T(2,128)}, f32[8,2,256]{2,1,0:T(2,128)S(1)}, u32[]{:S(2)}) copy-start(f32[8,2,256]{2,1,0:T(2,128)S(1)} %reshape.62.refs_4_) | copy-start | bytes 49156
  13.3 11.1 %copy-start.21 = (bf16[256,1024]{1,0:T(8,128)(2,1)S(1)}, bf16[256,1024]{1,0:T(8,128)(2,1)}, u32[]{:S(2)}) copy-start(bf16[256,1024]{1,0:T(8,128)(2,1)} %param.17) | copy-start | bytes 1572868
  21.8 10.1 %copy-start.4 = (f32[128,1024]{1,0:T(8,128)S(1)}, f32[128,1024]{1,0:T(8,128)}, u32[]{:S(2)}) copy-start(f32[128,1024]{1,0:T(8,128)} %get-tuple-element.23) | copy-start | bytes 1572868
  23.8 7.4 %collective-permute-start = (f32[136,1024]{1,0:T(8,128)S(1)}, f32[136,1024]{1,0:T(8,128)S(1)}, u32[]{:S(2)}, u32[]{:S(2)}) collective-permute-start(f32[136,1024]{1,0:T(8,128)S(1)} %pad_maximum_fusion.4), channel_id=1, source_target_pairs={{0,4},{4,0},{8,12},{12,8},{16,20},{20,16},{24,28},{28,24},{1,5},{5... | collective-permute-start | bytes 1671176 | tf_op jit(solution)/shard_map/ppermute | solution.py:112
  24.6 17.6 %collective-permute-start.5 = (bf16[256,1024]{0,1:T(8,128)(2,1)S(1)}, bf16[256,1024]{0,1:T(8,128)(2,1)S(1)}, u32[]{:S(2)}, u32[]{:S(2)}) collective-permute-start(bf16[256,1024]{0,1:T(8,128)(2,1)S(1)} %copy.51), channel_id=1, source_target_pairs={{3,0},{0,1},{1,2},{2,3},{7,4},{4,5},{5,6},{6,7},{11,8},{8,9},{9,10... | collective-permute-start | bytes 1572872 | tf_op jit(solution)/shard_map/ppermute | solution.py:127
  27.2 37.3 %collective-permute-start.4 = (bf16[256,1024]{0,1:T(8,128)(2,1)S(1)}, bf16[256,1024]{0,1:T(8,128)(2,1)}, u32[]{:S(2)}, u32[]{:S(2)}) collective-permute-start(bf16[256,1024]{0,1:T(8,128)(2,1)S(1)} %copy.51), channel_id=1, source_target_pairs={{2,0},{3,1},{0,2},{1,3},{6,4},{7,5},{4,6},{5,7},{10,8},{11,9},{8,1... | collective-permute-start | bytes 1572872 | tf_op jit(solution)/shard_map/ppermute | solution.py:127
  29.8 34.7 %collective-permute-start.3 = (bf16[256,1024]{0,1:T(8,128)(2,1)S(1)}, bf16[256,1024]{0,1:T(8,128)(2,1)}, u32[]{:S(2)}, u32[]{:S(2)}) collective-permute-start(bf16[256,1024]{0,1:T(8,128)(2,1)S(1)} %copy.51), channel_id=1, source_target_pairs={{1,0},{2,1},{3,2},{0,3},{5,4},{6,5},{7,6},{4,7},{9,8},{10,9},{11,1... | collective-permute-start | bytes 1572872 | tf_op jit(solution)/shard_map/ppermute | solution.py:127
  31.1 33.4 %copy-start.15 = (f32[136,1024]{1,0:T(8,128)}, f32[136,1024]{1,0:T(8,128)S(1)}, u32[]{:S(2)}) copy-start(f32[136,1024]{1,0:T(8,128)S(1)} %collective-permute-done) | copy-start | bytes 1671172
  32.9 39.4 %collective-permute-start.1 = (f32[136,1024]{1,0:T(8,128)}, f32[136,1024]{1,0:T(8,128)}, u32[]{:S(2)}, u32[]{:S(2)}) collective-permute-start(f32[136,1024]{1,0:T(8,128)} %pad_maximum_fusion.5), channel_id=1, source_target_pairs={{0,8},{4,12},{8,0},{12,4},{16,24},{20,28},{24,16},{28,20},{1,9},{5... | collective-permute-start | bytes 1671176 | tf_op jit(solution)/shard_map/ppermute | solution.py:112
  66.2 1.7 copy-start.8
  66.2 10.8 %copy-start.7 = (bf16[1,256,1024]{1,2,0:T(8,128)(2,1)}, bf16[1,256,1024]{1,2,0:T(8,128)(2,1)S(1)}, u32[]{:S(2)}) copy-start(bf16[1,256,1024]{1,2,0:T(8,128)(2,1)S(1)} %get-tuple-element.78) | copy-start | bytes 1572868
  67.9 44.6 %all-to-all-start = ((bf16[256,8,512]{0,2,1:T(8,128)(2,1)}), bf16[256,8,512]{0,2,1:T(8,128)(2,1)}, u32[]{:S(2)}, u32[]{:S(2)}) async-start(bf16[256,8,512]{0,2,1:T(8,128)(2,1)} %pad_maximum_fusion.2), calls=%async_computation | async-start | bytes 4194304 | tf_op jit(solution)/shard_map/all_to_all | solution.py:151
  72.3 145.6 %all-gather.5.cloned.1.call-start = ((), (), s32[]{:S(2)}) async-start(), calls=%async_computation.2 | async-start | bytes 4718592 | tf_op jit(solution)/shard_map/all_gather | solution.py:207
  75.2 34.7 %collective-permute-start.2 = (f32[136,1024]{1,0:T(8,128)}, f32[136,1024]{1,0:T(8,128)}, u32[]{:S(2)}, u32[]{:S(2)}) collective-permute-start(f32[136,1024]{1,0:T(8,128)} %pad_maximum_fusion.6), channel_id=1, source_target_pairs={{0,16},{4,20},{8,24},{12,28},{16,0},{20,4},{24,8},{28,12},{1,17},{... | collective-permute-start | bytes 1671176 | tf_op jit(solution)/shard_map/ppermute | solution.py:112
  77.0 32.9 %copy-start.16 = (f32[136,1024]{1,0:T(8,128)S(1)}, f32[136,1024]{1,0:T(8,128)}, u32[]{:S(2)}) copy-start(f32[136,1024]{1,0:T(8,128)} %copy-done.15) | copy-start | bytes 1671172
  116.4 5.9 %copy-start.29 = (f32[1024]{0:T(1024)S(1)}, f32[1024]{0:T(1024)}, u32[]{:S(2)}) copy-start(f32[1024]{0:T(1024)} %param.15) | copy-start | bytes 12292
  116.4 5.9 %copy-start.9 = (f32[256,1024]{1,0:T(8,128)S(1)}, f32[256,1024]{1,0:T(8,128)}, u32[]{:S(2)}) copy-start(f32[256,1024]{1,0:T(8,128)} %get-tuple-element.22) | copy-start | bytes 3145732
  116.4 5.9 %copy-start.18 = (f32[1024,256]{0,1:T(8,128)S(1)}, f32[1024,256]{0,1:T(8,128)}, u32[]{:S(2)}) copy-start(f32[1024,256]{0,1:T(8,128)} %fusion.66) | copy-start | bytes 3145732
  116.4 6.0 %copy-start.19 = (bf16[256,1024]{1,0:T(8,128)(2,1)S(1)}, bf16[256,1024]{1,0:T(8,128)(2,1)}, u32[]{:S(2)}) copy-start(bf16[256,1024]{1,0:T(8,128)(2,1)} %param.10) | copy-start | bytes 1572868
  116.4 6.0 %copy-start.30 = (f32[256,1024]{1,0:T(8,128)S(1)}, f32[256,1024]{1,0:T(8,128)}, u32[]{:S(2)}) copy-start(f32[256,1024]{1,0:T(8,128)} %get-tuple-element.21) | copy-start | bytes 3145732
  122.3 1.0 copy-start.11
  122.4 22.0 %copy-start.20 = (bf16[256,1024]{1,0:T(8,128)(2,1)S(1)}, bf16[256,1024]{1,0:T(8,128)(2,1)}, u32[]{:S(2)}) copy-start(bf16[256,1024]{1,0:T(8,128)(2,1)} %param.10) | copy-start | bytes 1572868
  148.8 2.0 copy-start.1
  148.8 102.0 %all-reduce.2.cloned.1.call-start = ((), (), s32[]{:S(2)}) async-start(), calls=%async_computation.3 | async-start | bytes 524288 | tf_op jit(solution)/shard_map/psum | solution.py:251
  149.1 45.8 %copy-start.26 = (pred[1024]{0:T(1024)(128)(4,1)}, pred[1024]{0:T(1024)(128)(4,1)S(1)}, u32[]{:S(2)}) copy-start(pred[1024]{0:T(1024)(128)(4,1)S(1)} %fusion.56) | copy-start | bytes 3076
  153.0 9.3 %copy-start.13 = (bf16[256,128]{1,0:T(8,128)(2,1)S(1)}, bf16[256,128]{1,0:T(8,128)(2,1)}, u32[]{:S(2)}) copy-start(bf16[256,128]{1,0:T(8,128)(2,1)} %refs_1_.1) | copy-start | bytes 196612
  153.0 11.7 %collective-permute-start.6 = (f32[136,1024]{1,0:T(8,128)}, f32[136,1024]{1,0:T(8,128)}, u32[]{:S(2)}, u32[]{:S(2)}) collective-permute-start(f32[136,1024]{1,0:T(8,128)} %pad_maximum_fusion.3), channel_id=1, source_target_pairs={{0,4},{4,0},{8,12},{12,8},{16,20},{20,16},{24,28},{28,24},{1,5},{5... | collective-permute-start | bytes 1671176 | tf_op jit(solution)/shard_map/ppermute | solution.py:112
  162.2 6.0 %copy-start.10 = (f32[256,256]{1,0:T(8,128)S(1)}, f32[256,256]{1,0:T(8,128)}, u32[]{:S(2)}) copy-start(f32[256,256]{1,0:T(8,128)} %get-tuple-element.27) | copy-start | bytes 786436
  166.6 26.3 %collective-permute-start.7 = (f32[136,1024]{1,0:T(8,128)S(1)}, f32[136,1024]{1,0:T(8,128)S(1)}, u32[]{:S(2)}, u32[]{:S(2)}) collective-permute-start(f32[136,1024]{1,0:T(8,128)S(1)} %pad_maximum_fusion.7), channel_id=1, source_target_pairs={{0,8},{4,12},{8,0},{12,4},{16,24},{20,28},{24,16},{28,20},{1,9},{5... | collective-permute-start | bytes 1671176 | tf_op jit(solution)/shard_map/ppermute | solution.py:112
  168.7 25.8 %copy-start.6 = (bf16[256,1024]{1,0:T(8,128)(2,1)S(1)}, bf16[256,1024]{1,0:T(8,128)(2,1)}, u32[]{:S(2)}) copy-start(bf16[256,1024]{1,0:T(8,128)(2,1)} %get-tuple-element.70) | copy-start | bytes 1572868
  193.7 1.2 copy-start.2
  193.9 14.5 %copy-start.5 = (f32[128,1024]{1,0:T(8,128)S(1)}, f32[128,1024]{1,0:T(8,128)}, u32[]{:S(2)}) copy-start(f32[128,1024]{1,0:T(8,128)} %get-tuple-element.23) | copy-start | bytes 1572868
  193.9 14.5 %collective-permute-start.8 = (f32[136,1024]{1,0:T(8,128)S(1)}, f32[136,1024]{1,0:T(8,128)S(1)}, u32[]{:S(2)}, u32[]{:S(2)}) collective-permute-start(f32[136,1024]{1,0:T(8,128)S(1)} %pad_maximum_fusion.8), channel_id=1, source_target_pairs={{0,16},{4,20},{8,24},{12,28},{16,0},{20,4},{24,8},{28,12},{1,17},{... | collective-permute-start | bytes 1671176 | tf_op jit(solution)/shard_map/ppermute | solution.py:112
  209.9 1.2 copy-start.17
  211.2 3.1 %copy-start.3 = (bf16[256,1024]{1,0:T(8,128)(2,1)S(1)}, bf16[256,1024]{1,0:T(8,128)(2,1)}, u32[]{:S(2)}) copy-start(bf16[256,1024]{1,0:T(8,128)(2,1)} %refs_0_.3) | copy-start | bytes 1572868
  211.2 3.1 %copy-start.27 = (pred[1024]{0:T(1024)(128)(4,1)S(1)}, pred[1024]{0:T(1024)(128)(4,1)}, u32[]{:S(2)}) copy-start(pred[1024]{0:T(1024)(128)(4,1)} %copy-done.26) | copy-start | bytes 3076
  214.2 0.7 copy-start.24
  214.2 0.7 copy-start.25
  214.5 0.7 copy-start.31
  216.5 1.6 copy-start.14
  218.1 5.9 %copy-start.28 = (f32[1024]{0:T(1024)S(1)}, f32[1024]{0:T(1024)}, u32[]{:S(2)}) copy-start(f32[1024]{0:T(1024)} %get-tuple-element.75) | copy-start | bytes 12292
Sparse Core Ops, SparseCore 0:
  9.9 61.4 all-gather.2
  148.9 45.0 all-gather.4
  218.1 32.7 all-reduce.1
